TPU v7x, 32 devices: a whole 2x2x4 slice. The times are simulated.
32 devices in a mesh: band: 8 (over z, x), ga: 4 (over y, core).
Axes of the slice: x: 2, y: 2, z: 4, core: 2. Of those that a mesh axis runs over, the one named last changes fastest.
Arguments:
- elements: bfloat16 [2, 768, 2048], P(None, 'band', 'ga'), may hold values from -0.75 to 0.75
- screened: bfloat16 [2, 2, 2048, 2048], P(None, None, 'ga'), may hold values from -0.09375 to 0.09375
- energies: float32 [768], replicated, may hold values from -3 to 3
- freq_points: float32 [2], replicated, may hold values from -3 to 3
- freq_weights: float32 [2], replicated, may hold values from 0.5 to 2
- band_of_slot: int32 [768], replicated, may hold values from 0 to 767, each once
Outputs:
- sigma: float32 [2, 768, 768], P(None, 'band', 'ga')
Inputs may be any that keep to these rules, and one draw needn't show every extreme that they name: `band_of_slot`: each of 0 to 767 stands once.
All inputs are finite; a program needn't handle non-finite values.
Results may differ from a plain program's by a relative error of at most 0.0042.
Values may be sent and summed in bfloat16 or wider, within the bound.
No kernel may reach another device: no remote copies, remote signals or barrier semaphores. Data moves between devices by JAX's collectives and lax.ppermute only.
A program may use at most 128 MiB of HBM per device.

v0:
```python
import jax
import jax.numpy as jnp
from jax import lax
from jax.sharding import PartitionSpec as P


def make_left(block):
    flipped = jnp.stack([-block[1], block[0]])
    return jnp.stack([block, flipped])


def on_device(elements, screened, energies, freq_points, freq_weights, band_of_slot):
    bands = elements.shape[1]
    slot_energy = jnp.take(energies, band_of_slot)
    offset = slot_energy[None, :] - freq_points[:, None]
    screen = freq_weights[:, None] / (1.0 + 4.0 * offset * offset)
    own_start = lax.axis_index("band") * bands
    screen_own = lax.dynamic_slice_in_dim(screen, own_start, bands, 1)
    piece = lax.all_gather(elements, "ga", axis=2, tiled=True)
    real_side = jnp.stack([piece[0], -piece[1]])
    imag_side = jnp.stack([piece[1], piece[0]])
    sides = jnp.stack([real_side, imag_side])
    applied = jnp.einsum(
        "dcmk,wcgk->wdmg", sides, screened, preferred_element_type=jnp.float32
    ).astype(jnp.bfloat16)
    left_own = make_left(elements)
    pairs = jnp.einsum(
        "dcnk,wcmk->wdnm",
        left_own,
        lax.all_gather(applied, "band", axis=2, tiled=True),
        preferred_element_type=jnp.float32,
    )
    factor = 0.5 * (screen_own[:, :, None] + screen[:, None, :])
    partial_rows = jnp.sum(pairs * factor[:, None], axis=0)
    return lax.psum_scatter(partial_rows, "ga", scatter_dimension=2, tiled=True)


def solution(mesh):
    placed = (P(None, "band", "ga"), P(None, None, "ga", None), P(), P(), P(), P())
    return jax.shard_map(
        on_device, mesh=mesh, in_specs=placed, out_specs=P(None, "band", "ga"), check_vma=False
    )
```

profile of v0, /device:TPU:0, one launch (start us, length us, event | category | flops | bytes accessed | tf_op | source)
XLA Modules:
  0.0 121.1 jit_solution(2113868990376874802)
XLA Ops:
  6.5 0.0 copy-start
  6.5 0.0 all-gather.2.cloned.1.call-start
  6.5 10.4 %all_gather.6 = bf16[2,96,2048]{2,1,0:T(8,128)(2,1)S(1)} all-gather(bf16[2,96,512]{2,1,0:T(8,128)(2,1)} %param.6), channel_id=1, replica_groups=mesh['band'=8,'ga'=4] {'ga'}, dimensions={2}, use_global_device_ids=true | all-gather | bytes 983040 | tf_op jit(solution)/shard_map/all_gather | solution.py:19
  17.0 0.1 slice_negate_fusion.1
  17.1 0.1 maximum_bitcast_fusion.8
  17.2 0.0 copy-start.2
  17.2 7.0 %fusion.21 = bf16[2,2,96,512]{3,2,1,0:T(8,128)(2,1)} fusion(bf16[2,2,512,2048]{3,2,1,0:T(8,128)(2,1)} %param.7, bf16[1,2,96,2048]{3,2,1,0:T(8,128)(2,1)S(1)} %get-tuple-element.9, bf16[1,2,96,2048]{3,2,1,0:T(8,128)(2,1)S(1)} %get-tuple-element.8), kind=kOutput, calls=%fused_computation.13 | convolution fusion | flops 1613955072 | bytes 10354688 | tf_op jit(solution)/shard_map/dcmk,wcgk->wdmg/dot_general | solution.py:23
  24.2 0.0 copy-start.3
  24.2 0.0 copy-start.4
  24.2 0.0 copy-start.1
  24.2 0.0 all-gather.2.cloned.1.call-update
  24.3 0.0 reduce-scatter.4.cloned.1.call-start
  24.3 0.0 copy-done.2
  24.4 0.0 copy-done
  24.4 3.2 %gather_fusion = f32[768]{0:T(1024)S(1)} fusion(f32[768]{0:T(1024)S(1)} %copy-done, s32[1024]{0:T(1024)S(1)} %pad_clamp_fusion), kind=kCustom, calls=%fused_computation | custom fusion | bytes 9216 | tf_op jit(solution)/shard_map/jit(_take)/gather | solution.py:14
  27.6 0.0 copy-done.3
  27.6 0.0 copy-done.4
  27.6 0.1 fusion.27
  27.7 0.1 constant_dynamic-slice_fusion
  27.8 0.0 copy-done.1
  27.8 0.1 add_multiply_fusion
  27.9 57.3 %all-gather.2.cloned.1.call-done = bf16[2,2,768,512]{3,2,1,0:T(8,128)(2,1)} async-done(((bf16[2,2,96,512]{3,2,1,0:T(8,128)(2,1)}), bf16[2,2,768,512]{3,2,1,0:T(8,128)(2,1)}) %all-gather.2.cloned.1.call-update) | async-done | bytes 3145744 | tf_op jit(solution)/shard_map/all_gather | solution.py:30
  85.3 3.1 %fusion.12 = f32[2,96,768]{2,1,0:T(8,128)S(1)} fusion(bf16[2,2,768,512]{3,2,1,0:T(8,128)(2,1)} %all-gather.2.cloned.1.call-done, f32[2,96,768]{2,1,0:T(8,128)S(1)} %add_multiply_fusion, bf16[1,2,96,512]{3,2,1,0:T(8,128)(2,1)S(1)} %maximum_bitcast_fusion.12, bf16[1,2,96,512]{3,2,1,0:T(8,128)(2,1)S(1)} %bitcast.63), kind=kOutput, calls=%fused_computation.10 | convolution fusion | flops 605208576 | bytes 4718592 | tf_op jit(solution)/shard_map/dcnk,wcmk->wdnm/dot_general | solution.py:27
  88.4 0.5 copy.11
  88.9 1.4 %reshape.63 = f32[768,192]{1,0:T(8,128)} reshape(f32[768,2,96]{2,1,0:T(2,128)S(1)} %bitcast.61) | data formatting | bytes 1179648
  90.2 0.0 reduce-scatter.4.cloned.1.call-update
  90.3 22.0 %reduce-scatter.4.cloned.1.call-done = f32[192,192]{1,0:T(8,128)} async-done(((f32[768,192]{1,0:T(8,128)}), f32[192,192]{1,0:T(8,128)}) %reduce-scatter.4.cloned.1.call-update) | async-done | bytes 147472
  112.3 1.1 reshape.64
  113.4 0.8 copy.12
  (5 shorter events, 0.1 us)
Async XLA Ops:
  6.5 17.8 %copy-start = (f32[768]{0:T(1024)S(1)}, f32[768]{0:T(1024)}, u32[]{:S(2)}) copy-start(f32[768]{0:T(1024)} %param.8) | copy-start | bytes 9220
  6.5 78.7 %all-gather.2.cloned.1.call-start = ((), (), s32[]{:S(2)}) async-start(), calls=%async_computation.1 | async-start | bytes 3538944 | tf_op jit(solution)/shard_map/all_gather | solution.py:30
  17.2 7.1 %copy-start.2 = (s32[768]{0:T(1024)S(1)}, s32[768]{0:T(1024)}, u32[]{:S(2)}) copy-start(s32[768]{0:T(1024)} %param.11) | copy-start | bytes 9220
  24.2 3.3 %copy-start.3 = (f32[2]{0:T(128)S(1)}, f32[2]{0:T(128)}, u32[]{:S(2)}) copy-start(f32[2]{0:T(128)} %param.10) | copy-start | bytes 28
  24.2 3.4 %copy-start.4 = (f32[2]{0:T(128)S(1)}, f32[2]{0:T(128)}, u32[]{:S(2)}) copy-start(f32[2]{0:T(128)} %param.9) | copy-start | bytes 28
  24.2 3.5 %copy-start.1 = (bf16[2,96,512]{2,1,0:T(8,128)(2,1)S(1)}, bf16[2,96,512]{2,1,0:T(8,128)(2,1)}, u32[]{:S(2)}) copy-start(bf16[2,96,512]{2,1,0:T(8,128)(2,1)} %param.6) | copy-start | bytes 589828
  24.3 88.0 %reduce-scatter.4.cloned.1.call-start = ((), (), s32[]{:S(2)}) async-start(), calls=%async_computation.2 | async-start | bytes 983040
Sparse Core Ops, SparseCore 0:
  24.4 60.8 all-gather.1
  90.4 21.8 reduce-scatter.3
where the time goes:
time: 121 us
  waiting for transfers between devices  79.4 us (66%)
  between operations  13.5 us (11%)
  blocking collectives  10.4 us (9%)
  matrix products  10.2 us (8%)
  local copies, waits for them, and re-layouts  7.04 us (6%)
    all_gather x1, waiting for transfers between devices, on_device(): lax.all_gather(applied, 'band', axis=2, tiled=True)  57.3 us
    unnamed x3, waiting for transfers between devices  22.1 us
    all_gather x1, blocking collectives, on_device(): piece = lax.all_gather(elements, 'ga', axis=2, tiled=True)  10.4 us
    dot_general x1, matrix products, on_device(): jnp.einsum('dcmk,wcgk->wdmg', sides, screened, preferred_element_type=jnp...  7.03 us
    unnamed x14, local copies, waits for them, and re-layouts  3.77 us
    gather x1, local copies, waits for them, and re-layouts, on_device(): slot_energy = jnp.take(energies, band_of_slot)  3.19 us
    dot_general x1, matrix products, on_device(): jnp.einsum('dcnk,wcmk->wdnm', left_own, lax.all_gather(applied, 'band', a...  3.12 us
  transfers between devices with their start and end apart: 2, of which 2 were waited for; matrix products, arithmetic and copies ran while one was open for 3% of the time, Pallas kernels for 0%

commit v1 on v0

--- a/solution.py
+++ b/solution.py
@@ -27,7 +27,9 @@
     pairs = jnp.einsum(
         "dcnk,wcmk->wdnm",
         left_own,
-        lax.all_gather(applied, "band", axis=2, tiled=True),
+        jnp.concatenate(
+            lax.all_to_all(jnp.stack([applied] * lax.axis_size("band")), "band", 0, 0), axis=2
+        ),
         preferred_element_type=jnp.float32,
     )
     factor = 0.5 * (screen_own[:, :, None] + screen[:, None, :])

time: 121 us -> 138 us (1.14)
  waiting for transfers between devices: 79.4 us -> 88.7 us
  starting transfers between devices: 0.04 us -> 5.98 us
  local copies, waits for them, and re-layouts: 7.04 us -> 10.1 us
  matrix products: 10.2 us -> 7.46 us
    all_to_all x0 -> x1, waiting for transfers between devices: none -> 66.7 us  [on_device(): lax.all_to_all(jnp.stack([applied] * lax.axis_size('band')), 'band', 0, 0)]
    all_gather x1 -> x0, waiting for transfers between devices: 57.3 us -> none  [on_device(): lax.all_gather(applied, 'band', axis=2, tiled=True)]
    all_to_all x0 -> x1, starting transfers between devices: none -> 5.94 us  [on_device(): lax.all_to_all(jnp.stack([applied] * lax.axis_size('band')), 'band', 0, 0)]
    another operation x0 -> x1, local copies, waits for them, and re-layouts: none -> 2 us  [on_device(): jnp.stack([applied] * lax.axis_size('band'))]
    dot_general x1, matrix products: 3.12 us -> 1.18 us  [on_device(): jnp.einsum('dcnk,wcmk->wdnm', left_own, jnp.concatenate(lax.all_to_all(jn...]
    unnamed x14 -> x16, local copies, waits for them, and re-layouts: 3.77 us -> 4.58 us
    unnamed x3 -> x2, waiting for transfers between devices: 22.1 us -> 22 us
where the time goes in v1:
time: 138 us
  waiting for transfers between devices  88.7 us (64%)
  between operations  13.6 us (10%)
  blocking collectives  10.4 us (8%)
  local copies, waits for them, and re-layouts  10.1 us (7%)
  matrix products  7.46 us (5%)
  starting transfers between devices  5.98 us (4%)
    all_to_all x1, waiting for transfers between devices, on_device(): lax.all_to_all(jnp.stack([applied] * lax.axis_size('band')), 'band', 0, 0)  66.7 us
    unnamed x2, waiting for transfers between devices  22 us
    all_gather x1, blocking collectives, on_device(): piece = lax.all_gather(elements, 'ga', axis=2, tiled=True)  10.4 us
    dot_general x1, matrix products, on_device(): jnp.einsum('dcmk,wcgk->wdmg', sides, screened, preferred_element_type=jnp...  6.28 us
    all_to_all x1, starting transfers between devices, on_device(): lax.all_to_all(jnp.stack([applied] * lax.axis_size('band')), 'band', 0, 0)  5.94 us
    unnamed x16, local copies, waits for them, and re-layouts  4.58 us
    gather x1, local copies, waits for them, and re-layouts, on_device(): slot_energy = jnp.take(energies, band_of_slot)  3.19 us
  transfers between devices with their start and end apart: 2, of which 2 were waited for; matrix products, arithmetic and copies ran while one was open for 3% of the time, Pallas kernels for 0%

profile of v1, /device:TPU:0, one launch (start us, length us, event | category | flops | bytes accessed | tf_op | source)
XLA Modules:
  0.0 137.6 jit_solution(18008367494852614007)
XLA Ops:
  6.5 0.0 copy-start
  6.5 10.4 %all_gather.3 = bf16[2,96,2048]{2,1,0:T(8,128)(2,1)S(1)} all-gather(bf16[2,96,512]{2,1,0:T(8,128)(2,1)} %param.6), channel_id=1, replica_groups=mesh['band'=8,'ga'=4] {'ga'}, dimensions={2}, use_global_device_ids=true | all-gather | bytes 983040 | tf_op jit(solution)/shard_map/all_gather | solution.py:19
  17.0 0.1 slice_negate_fusion.1
  17.0 0.1 maximum_bitcast_fusion.8
  17.2 6.3 %fusion.12 = bf16[2,2,96,512]{3,2,0,1:T(8,128)(2,1)S(1)} fusion(bf16[2,2,512,2048]{3,2,1,0:T(8,128)(2,1)} %param.7, bf16[1,2,96,2048]{3,2,1,0:T(8,128)(2,1)S(1)} %get-tuple-element.9, bf16[1,2,96,2048]{3,2,1,0:T(8,128)(2,1)S(1)} %get-tuple-element.8), kind=kOutput, calls=%fused_computation.11 | convolution fusion | flops 1613955072 | bytes 10354688 | tf_op jit(solution)/shard_map/dcmk,wcgk->wdmg/dot_general | solution.py:23
  23.5 2.0 %stack.45 = bf16[8,2,2,96,512]{4,3,2,1,0:T(8,128)(2,1)} broadcast(bf16[2,2,96,512]{3,2,1,0:T(8,128)(2,1)S(1)} %copy.9), dimensions={1,2,3,4} | broadcast | bytes 3538944 | tf_op jit(solution)/shard_map/stack | solution.py:31
  25.5 0.0 copy-start.3
  25.5 5.9 %all-to-all-start = ((bf16[8,2,2,96,512]{4,3,2,1,0:T(8,128)(2,1)}), bf16[8,2,2,96,512]{4,3,2,1,0:T(8,128)(2,1)S(1)}, u32[]{:S(2)}, u32[]{:S(2)}) async-start(bf16[8,2,2,96,512]{4,3,2,1,0:T(8,128)(2,1)} %stack.45), calls=%async_computation | async-start | bytes 6291456 | tf_op jit(solution)/shard_map/all_to_all | solution.py:31
  31.5 0.0 copy-start.4
  31.5 0.0 copy-start.5
  31.5 0.0 copy-start.1
  31.5 0.0 reduce-scatter.4.cloned.1.call-start
  31.5 0.0 copy-done.3
  31.6 0.0 copy-done
  31.6 3.2 %gather_fusion = f32[768]{0:T(1024)S(1)} fusion(f32[768]{0:T(1024)S(1)} %copy-done, s32[1024]{0:T(1024)S(1)} %pad_clamp_fusion), kind=kCustom, calls=%fused_computation | custom fusion | bytes 9216 | tf_op jit(solution)/shard_map/jit(_take)/gather | solution.py:14
  34.8 0.0 copy-done.4
  34.8 0.0 copy-done.5
  34.8 0.1 fusion.18
  34.9 0.1 constant_dynamic-slice_fusion
  35.0 0.0 copy-done.1
  35.0 0.9 add_multiply_fusion
  36.0 66.7 %all-to-all-done = bf16[8,2,2,96,512]{4,3,2,1,0:T(8,128)(2,1)S(1)} async-done(((bf16[8,2,2,96,512]{4,3,2,1,0:T(8,128)(2,1)}), bf16[8,2,2,96,512]{4,3,2,1,0:T(8,128)(2,1)S(1)}, u32[]{:S(2)}, u32[]{:S(2)}) %all-to-all-start) | async-done | bytes 3145760 | tf_op jit(solution)/shard_map/all_to_all | solution.py:31
  102.7 0.0 copy-start.2
  102.7 0.2 copy.10
  102.9 0.8 copy-done.2
  103.7 1.2 fusion.5
  104.9 0.5 copy.15
  105.4 1.4 reshape.73
  106.8 0.0 reduce-scatter.4.cloned.1.call-update
  106.8 22.0 %reduce-scatter.4.cloned.1.call-done = f32[192,192]{1,0:T(8,128)} async-done(((f32[768,192]{1,0:T(8,128)}), f32[192,192]{1,0:T(8,128)}) %reduce-scatter.4.cloned.1.call-update) | async-done | bytes 147472
  128.8 1.1 reshape.74
  129.9 0.8 copy.16
  (6 shorter events, 0.1 us)
Async XLA Ops:
  6.5 25.0 %copy-start = (f32[768]{0:T(1024)S(1)}, f32[768]{0:T(1024)}, u32[]{:S(2)}) copy-start(f32[768]{0:T(1024)} %param.8) | copy-start | bytes 9220
  25.5 6.0 %copy-start.3 = (s32[768]{0:T(1024)S(1)}, s32[768]{0:T(1024)}, u32[]{:S(2)}) copy-start(s32[768]{0:T(1024)} %param.11) | copy-start | bytes 9220
  25.5 77.2 %all-to-all-start = ((bf16[8,2,2,96,512]{4,3,2,1,0:T(8,128)(2,1)}), bf16[8,2,2,96,512]{4,3,2,1,0:T(8,128)(2,1)S(1)}, u32[]{:S(2)}, u32[]{:S(2)}) async-start(bf16[8,2,2,96,512]{4,3,2,1,0:T(8,128)(2,1)} %stack.45), calls=%async_computation | async-start | bytes 6291456 | tf_op jit(solution)/shard_map/all_to_all | solution.py:31
  31.5 3.3 %copy-start.4 = (f32[2]{0:T(128)S(1)}, f32[2]{0:T(128)}, u32[]{:S(2)}) copy-start(f32[2]{0:T(128)} %param.10) | copy-start | bytes 28
  31.5 3.3 %copy-start.5 = (f32[2]{0:T(128)S(1)}, f32[2]{0:T(128)}, u32[]{:S(2)}) copy-start(f32[2]{0:T(128)} %param.9) | copy-start | bytes 28
  31.5 3.5 %copy-start.1 = (bf16[2,96,512]{2,1,0:T(8,128)(2,1)S(1)}, bf16[2,96,512]{2,1,0:T(8,128)(2,1)}, u32[]{:S(2)}) copy-start(bf16[2,96,512]{2,1,0:T(8,128)(2,1)} %param.6) | copy-start | bytes 589828
  31.5 97.3 %reduce-scatter.4.cloned.1.call-start = ((), (), s32[]{:S(2)}) async-start(), calls=%async_computation.2 | async-start | bytes 983040
  102.7 1.1 copy-start.2
Sparse Core Ops, SparseCore 0:
  106.9 21.8 reduce-scatter.3
